TPU v7x, 32 devices: a whole 2x2x4 slice. The times are simulated.
32 devices in a mesh: ta: 8 (over y, x, core), sa: 4 (over z).
Axes of the slice: x: 2, y: 2, z: 4, core: 2. Of those that a mesh axis runs over, the one named last changes fastest.
Arguments:
- eigenvectors: bfloat16 [8, 256, 2, 3, 4, 384], P('ta', None, None, None, 'sa'), may hold values from -17 to 17
- momenta: int32 [8, 3], replicated, may hold values from -4 to 4
- block_order: int32 [4], replicated, may hold values from 0 to 3, each once
Outputs:
- meson_fields: float32 [8, 16, 64, 8, 128], P(None, 'sa', 'ta')
- slice_norms: float32 [8, 256], P('ta')
Inputs may be any that keep to these rules, and one draw needn't show every extreme that they name: block_order names every block once.
All inputs are finite; a program needn't handle non-finite values.
Results may differ from a plain program's by a relative error of at most 0.0018.
Values sent between devices are 32-bit elements; how exact they have to be, the bound alone decides.
A program may use at most 64 MiB of HBM per device.

v0:
```python
import functools
import math

import jax
import jax.numpy as jnp
from jax import lax
from jax.experimental import pallas as pl
from jax.experimental.pallas import tpu as pltpu
from jax.sharding import PartitionSpec as P

NC = 3
BS = 64
NBLK = 4
LX = 96
MESH = pl.DeviceIdType.MESH

full_turn = 2.0 * math.pi


def kernel(
    n, nta, scale, inv_count,
    order_ref, momenta_ref, ev_ref,
    out_ref, norm_ref,
    left, right, parts, rbuf, lbuf, final, recv, nbuf,
    rsend, rrecv, lsend, lrecv, asend, arecv, nsend, nrecv,
):
    t, z = lax.axis_index("ta"), lax.axis_index("sa")
    moms, planes = momenta_ref.shape[1], ev_ref.shape[-1]
    ppd = NBLK * NBLK // n
    rows = BS // nta
    half = NC * planes

    barrier = pltpu.get_barrier_semaphore()
    for j in range(1, n):
        pl.semaphore_signal(barrier, inc=1, device_id={"sa": lax.rem(z + j, n)}, device_id_type=MESH)
    for j in range(1, nta):
        pl.semaphore_signal(barrier, inc=1, device_id={"ta": lax.rem(t + j, nta)}, device_id_type=MESH)

    for b in range(NBLK):
        stored = order_ref[b]
        for k in range(2 * NC):
            left[b * BS:(b + 1) * BS, k * planes:(k + 1) * planes] = ev_ref[k, stored]
    def norm_copy(peer, slot):
        return pltpu.make_async_remote_copy(
            src_ref=nbuf.at[slot], dst_ref=nbuf.at[slot], send_sem=nsend.at[peer], recv_sem=nrecv.at[slot],
            device_id={"sa": peer}, device_id_type=MESH,
        )

    def shard(ref, p, s):
        return ref.at[p, pl.ds(s * ppd, ppd)]

    def rightward(src, p, s):
        return pltpu.make_async_remote_copy(
            src_ref=shard(src, p, s), dst_ref=shard(rbuf, p, s), send_sem=rsend.at[p, s], recv_sem=rrecv.at[p, s],
            device_id={"sa": lax.rem(z + 1, n)}, device_id_type=MESH,
        )

    def leftward(src, p, s):
        return pltpu.make_async_remote_copy(
            src_ref=shard(src, p, s), dst_ref=shard(lbuf, p, s), send_sem=lsend.at[p, s], recv_sem=lrecv.at[p, s],
            device_id={"sa": lax.rem(z + n - 1, n)}, device_id_type=MESH,
        )

    def compute(p):
        site = lax.broadcasted_iota(jnp.int32, (1, planes), 1)
        phase_index = (
            momenta_ref[0, p] * lax.rem(site, LX)
            + momenta_ref[1, p] * lax.div(site, LX)
            + momenta_ref[2, p] * z
        )
        angles = jnp.mod(phase_index, LX).astype(jnp.float32) * (full_turn / LX)
        cosine, sine = jnp.cos(angles), jnp.sin(angles)
        for c in range(NC):
            lanes = slice(c * planes, (c + 1) * planes)
            upper = slice(half + c * planes, half + (c + 1) * planes)
            for b in range(NBLK):
                re = left[b * BS:(b + 1) * BS, lanes].astype(jnp.float32)
                im = left[b * BS:(b + 1) * BS, upper].astype(jnp.float32)
                phased_re = (re * cosine + im * sine).astype(jnp.bfloat16)
                phased_im = (im * cosine - re * sine).astype(jnp.bfloat16)
                first = slice(2 * b * BS, (2 * b + 1) * BS)
                second = slice((2 * b + 1) * BS, (2 * b + 2) * BS)
                right[first, lanes] = phased_re
                right[first, upper] = phased_im
                right[second, lanes] = phased_im
                right[second, upper] = -phased_re
        for pair in range(NBLK // 2):
            product = lax.dot_general(
                left[...], right[pair * 4 * BS:(pair + 1) * 4 * BS, :], (((1,), (1,)), ((), ())),
                preferred_element_type=jnp.float32,
            )
            for a in range(NBLK):
                for b in range(2):
                    parts[p, a * NBLK + 2 * pair + b] = product[a * BS:(a + 1) * BS, b * 2 * BS:(b + 1) * 2 * BS]

    def open_lines(slot):
        @pl.when(z == 0)
        def _():
            for s in range(n - 1, 0, -1):
                p = slot - (n - 1 - s)

                @pl.when((p >= 0) & (p < moms))
                def _():
                    rightward(parts, p, s).start()

        @pl.when(z == n - 1)
        def _():
            for s in range(n - 1):
                p = slot - s

                @pl.when((p >= 0) & (p < moms))
                def _():
                    leftward(parts, p, s).start()

    def compute_and_open(p, carry):
        compute(p)
        open_lines(p)
        return carry

    def only_open(slot, carry):
        open_lines(slot)
        return carry

    compute(0)
    pl.semaphore_wait(barrier, n - 1 + nta - 1)
    open_lines(0)
    lax.fori_loop(1, moms, compute_and_open, 0)
    lax.fori_loop(moms, moms + n - 2, only_open, 0)

    squares = []
    for b in range(NBLK):
        total = jnp.zeros((BS, 128), jnp.float32)
        for k in range(2 * NC):
            for lane in range(0, planes, 128):
                value = ev_ref[k, b, :, lane:lane + 128].astype(jnp.float32)
                total = total + value * value
        squares.append(total)
    nbuf[z] = lax.dot_general(
        jnp.ones((8, 128), jnp.float32), jnp.concatenate(squares, axis=0), (((1,), (1,)), ((), ())),
        precision=lax.Precision.HIGHEST, preferred_element_type=jnp.float32,
    )

    for j in range(1, n):
        norm_copy(lax.rem(z + j, n), z).start()

    def rows_copy(p, peer):
        return pltpu.make_async_remote_copy(
            src_ref=final.at[p, peer], dst_ref=recv.at[p, t], send_sem=asend.at[p], recv_sem=arecv.at[p],
            device_id={"ta": peer}, device_id_type=MESH,
        )

    def step(i, carry):
        p_final = i - (n - 2)
        p_out = p_final - 1

        for s in range(n - 1, 0, -1):
            p_right = i - (z - 1) - (n - 1 - s)

            @pl.when((z > 0) & (s > z) & (p_right >= 0) & (p_right < moms))
            def _():
                copy = rightward(rbuf, p_right, s)
                copy.wait_recv()
                for k in range(ppd):
                    rbuf[p_right, s * ppd + k] += parts[p_right, s * ppd + k]
                copy.start()

        for s in range(n - 1):
            p_left = i - (n - 2 - z) - s

            @pl.when((z < n - 1) & (s < z) & (p_left >= 0) & (p_left < moms))
            def _():
                copy = leftward(lbuf, p_left, s)
                copy.wait_recv()
                for k in range(ppd):
                    lbuf[p_left, s * ppd + k] += parts[p_left, s * ppd + k]
                copy.start()

        @pl.when((p_final >= 0) & (p_final < moms))
        def _():
            @pl.when(z > 0)
            def _():
                rightward(rbuf, p_final, z).wait_recv()
                for k in range(ppd):
                    parts[p_final, z * ppd + k] += rbuf[p_final, z * ppd + k]

            @pl.when(z < n - 1)
            def _():
                leftward(lbuf, p_final, z).wait_recv()
                for k in range(ppd):
                    parts[p_final, z * ppd + k] += lbuf[p_final, z * ppd + k]

            for k in range(ppd):
                value = parts[p_final, z * ppd + k] * scale
                for peer in range(nta):
                    final[p_final, peer, k] = value[peer * rows:(peer + 1) * rows]
            for j in range(1, nta):
                rows_copy(p_final, lax.rem(t + j, nta)).start()
            recv[p_final, t] = final[p_final, t]

        @pl.when((p_out >= 0) & (p_out < moms))
        def _():
            arrived = recv.at[p_out, pl.ds(0, nta - 1)]
            pltpu.make_async_copy(arrived, arrived, arecv.at[p_out]).wait()
            for source in range(nta):
                for k in range(ppd):
                    out_ref[p_out, k, :, source, :] = recv[p_out, source, k]

        return carry

    lax.fori_loop(0, moms + n - 1, step, 0)

    for j in range(1, n):
        norm_copy(lax.rem(z + j, n), lax.rem(z + j, n)).wait_recv()
    total = nbuf[0]
    for q in range(1, n):
        total = total + nbuf[q]
    norm_ref[...] = total[0:1] * inv_count
    for j in range(1, n):
        norm_copy(lax.rem(z + j, n), z).wait_send()

    def drain(p, carry):
        for s in range(n):
            @pl.when(s > z)
            def _():
                rightward(parts, p, s).wait_send()

            @pl.when(s < z)
            def _():
                leftward(parts, p, s).wait_send()
        sent = final.at[p, pl.ds(0, nta - 1)]
        pltpu.make_async_copy(sent, sent, asend.at[p]).wait()
        return carry

    lax.fori_loop(0, moms, drain, 0)


def body(eigenvectors, momenta, block_order):
    planes = eigenvectors.shape[-1]
    n, nta = lax.axis_size("sa"), lax.axis_size("ta")
    moms = momenta.shape[0]
    nv = eigenvectors.shape[1]
    ppd = NBLK * NBLK // n
    rows = BS // nta
    stored = eigenvectors.reshape(NBLK, BS, 2 * NC, planes).transpose(2, 0, 1, 3)
    count = 2 * NC * n * planes
    f32 = jnp.float32
    vmem = pl.BlockSpec(memory_space=pltpu.VMEM)
    smem = pl.BlockSpec(memory_space=pltpu.SMEM)
    dma = pltpu.SemaphoreType.DMA
    fields, norms = pl.pallas_call(
        functools.partial(kernel, n, nta, 1.0 / math.sqrt(count), 1.0 / count),
        out_shape=(
            jax.ShapeDtypeStruct((moms, ppd, rows, nta, 2 * BS), f32),
            jax.ShapeDtypeStruct((1, nv), f32),
        ),
        in_specs=[smem, smem, vmem],
        out_specs=(vmem, vmem),
        scratch_shapes=[
            pltpu.VMEM((nv, 2 * NC * planes), jnp.bfloat16),
            pltpu.VMEM((2 * nv, 2 * NC * planes), jnp.bfloat16),
            pltpu.VMEM((moms, NBLK * NBLK, BS, 2 * BS), f32),
            pltpu.VMEM((moms, NBLK * NBLK, BS, 2 * BS), f32),
            pltpu.VMEM((moms, NBLK * NBLK, BS, 2 * BS), f32),
            pltpu.VMEM((moms, nta, ppd, rows, 2 * BS), f32),
            pltpu.VMEM((moms, nta, ppd, rows, 2 * BS), f32),
            pltpu.VMEM((n, 8, nv), f32),
            dma((moms, n)), dma((moms, n)), dma((moms, n)), dma((moms, n)),
            dma((moms,)), dma((moms,)), dma((n,)), dma((n,)),
        ],
        compiler_params=pltpu.CompilerParams(collective_id=0, has_side_effects=True, vmem_limit_bytes=30 * 1024 * 1024),
    )(block_order, momenta.T, stored)
    return fields, norms


def solution(mesh):
    return jax.shard_map(
        body,
        mesh=mesh,
        in_specs=(P("ta", None, None, None, "sa", None), P(), P()),
        out_specs=(P(None, "sa", "ta", None, None), P("ta", None)),
        check_vma=False,
    )
```

profile of v0, /device:TPU:0, one launch (start us, length us, event | category | flops | bytes accessed | tf_op | source)
XLA Modules:
  0.0 83.5 jit_solution(15953533911063074427)
XLA Ops:
  0.6 0.0 copy-start
  0.6 0.0 copy-start.1
  0.6 1.4 %copy.5 = bf16[1,256,2,3,1,384]{5,1,3,2,4,0:T(8,128)(2,1)S(1)} copy(bf16[1,256,2,3,1,384]{5,2,4,3,1,0:T(2,128)(2,1)} %param.3) | data formatting | bytes 2359296 | tf_op args[0]
  2.1 0.0 copy-done
  2.1 0.0 copy-done.1
  2.1 79.8 %shard_map.50 = (f32[8,4,8,8,128]{4,3,2,1,0:T(8,128)S(1)}, f32[1,256]{1,0:T(1,128)S(1)}) custom-call(s32[4]{0:T(128)S(1)} %copy-done.1, s32[3,8]{1,0:T(4,128)S(1)} %bitcast.5, bf16[6,4,64,384]{3,2,1,0:T(8,128)(2,1)S(1)} %bitcast.4), custom_call_target="tpu_custom_call" | custom-call | tf_op jit(solution)/shard_map/pallas_call | solution.py:250
  81.9 1.0 %copy.8 = f32[8,4,8,8,128]{4,3,2,1,0:T(8,128)} copy(f32[8,4,8,8,128]{4,3,2,1,0:T(8,128)S(1)} %get-tuple-element.4) | data formatting | bytes 2097152
  82.9 0.6 copy.9
Async XLA Ops:
  0.6 1.5 %copy-start = (s32[8,3]{0,1:T(4,128)S(1)}, s32[8,3]{0,1:T(4,128)}, u32[]{:S(2)}) copy-start(s32[8,3]{0,1:T(4,128)} %param.4) | copy-start | bytes 292
  0.6 1.5 %copy-start.1 = (s32[4]{0:T(128)S(1)}, s32[4]{0:T(128)}, u32[]{:S(2)}) copy-start(s32[4]{0:T(128)} %order_ref.1) | copy-start | bytes 52
where the time goes:
time: 83.6 us; the launch traced here: 83.5 us
  Pallas kernels  79.8 us (95%)
  local copies, waits for them, and re-layouts  2.98 us (4%)
    pallas_call x1, Pallas kernels, body(): pl.pallas_call(functools.partial(kernel, n, nta, 1.0 / math.sqrt(count),...  79.8 us
    unnamed x7, local copies, waits for them, and re-layouts  2.98 us

commit v1 on v0

--- a/solution.py
+++ b/solution.py
@@ -17,7 +17,7 @@
 full_turn = 2.0 * math.pi
 
 
-def kernel(
+def line_kernel(
     n, nta, scale, inv_count,
     order_ref, momenta_ref, ev_ref,
     out_ref, norm_ref,
@@ -234,6 +234,478 @@
     lax.fori_loop(0, moms, drain, 0)
 
 
+GV = 16
+
+
+def pair_kernel(
+    n, nta, scale, inv_count,
+    order_ref, momenta_ref, ev_ref,
+    out_ref, norm_ref,
+    lown, lend, rown, rend, trig, vsend, vrecv, field, rbuf, ebuf, fin, recv, nbuf,
+    vss, vrs, msend, mrecv, arecv, brecv, fsend, frecv, xsend, xrecv, nsend, nrecv,
+):
+    t, z = lax.axis_index("ta"), lax.axis_index("sa")
+    moms, planes = momenta_ref.shape[1], ev_ref.shape[-1]
+    half = NC * planes
+    ng = BS // GV
+    groups = NBLK * ng
+    first_groups = groups // 2
+    tile = 2 * GV
+    wide = 2 * BS
+    rows = BS // nta
+    per = GV // rows
+    hi = z // (n // 2)
+    end_id = hi * (n - 1)
+    mid_id = 1 + hi * (n - 3)
+    other_id = n - 1 - z
+
+    def blk(m, h):
+        return m + h * (NBLK - 1 - 2 * m)
+
+    def first(s, h):
+        return blk(NBLK - 1 - lax.rem(s, 2), h) * ng + s // 2
+
+    def second(s, h):
+        return blk(NBLK - 1 - s // ng, h) * ng + lax.rem(s, ng)
+
+    def at(start, size, step):
+        return pl.ds(pl.multiple_of(start, step), size)
+
+    row0, row1 = blk(0, hi) * wide, blk(1, hi) * wide
+    row3 = blk(NBLK - 1, hi) * wide
+    row2 = blk(NBLK - 2, hi) * wide
+    far = (1 - hi) * 2 * wide
+    rel3, rel2 = (1 - hi) * wide, hi * wide
+    got0, got1 = hi * wide, (1 - hi) * wide
+
+    barrier = pltpu.get_barrier_semaphore()
+    for j in range(1, n):
+        pl.semaphore_signal(barrier, inc=1, device_id={"sa": lax.rem(z + j, n)}, device_id_type=MESH)
+    for j in range(1, nta):
+        pl.semaphore_signal(barrier, inc=1, device_id={"ta": lax.rem(t + j, nta)}, device_id_type=MESH)
+
+    def remote(src, dst, send_sem, recv_sem, peer):
+        return pltpu.make_async_remote_copy(
+            src_ref=src, dst_ref=dst, send_sem=send_sem, recv_sem=recv_sem,
+            device_id={"sa": peer}, device_id_type=MESH,
+        )
+
+    def vector_copy(s):
+        return remote(vsend.at[s], vrecv.at[s], vss.at[s], vrs.at[s], mid_id)
+
+    def tile_copy(slot, group, rel):
+        return remote(
+            field.at[group, at(far + rel, tile, tile)], rbuf.at[group, at(rel, tile, tile)],
+            msend.at[slot], mrecv.at[lax.rem(slot, first_groups)], other_id,
+        )
+
+    def a_copy(s, group, row, rel):
+        return remote(
+            field.at[group, at(row, wide, wide)], rbuf.at[group, at(rel, wide, wide)],
+            msend.at[s], arecv.at[s - first_groups], other_id,
+        )
+
+    def b_copy(s, group, row, rel):
+        return remote(
+            field.at[group, at(row, wide, wide)], rbuf.at[group, at(rel, wide, wide)],
+            msend.at[s], brecv.at[s - first_groups], other_id,
+        )
+
+    def forward_copy(slot, group):
+        return remote(field.at[group, at(row0, wide, wide)], ebuf.at[group], fsend.at[slot], frecv.at[slot], end_id)
+
+    def norm_copy(peer, slot):
+        return remote(nbuf.at[slot], nbuf.at[slot], nsend.at[peer], nrecv.at[slot], peer)
+
+    def rows_copy(group, peer):
+        return pltpu.make_async_remote_copy(
+            src_ref=fin.at[group, peer // per, :, lax.rem(peer, per)], dst_ref=recv.at[group, t],
+            send_sem=xsend.at[group], recv_sem=xrecv.at[group],
+            device_id={"ta": peer}, device_id_type=MESH,
+        )
+
+    def angles(slot, plane):
+        site = lax.broadcasted_iota(jnp.int32, (1, planes), 1)
+        for p in range(moms):
+            phase_index = (
+                momenta_ref[0, p] * lax.rem(site, LX)
+                + momenta_ref[1, p] * lax.div(site, LX)
+                + momenta_ref[2, p] * plane
+            )
+            angle = jnp.mod(phase_index, LX).astype(jnp.float32) * (full_turn / LX)
+            trig[slot, 0, p:p + 1] = jnp.cos(angle)
+            trig[slot, 1, p:p + 1] = jnp.sin(angle)
+
+    def phased(load, slot, store):
+        for c in range(NC):
+            re, im = load(c), load(NC + c)
+            for p in range(moms):
+                cosine, sine = trig[slot, 0, p:p + 1], trig[slot, 1, p:p + 1]
+                store(p, c, (re * cosine + im * sine).astype(jnp.bfloat16))
+                store(p, NC + c, (im * cosine - re * sine).astype(jnp.bfloat16))
+
+    def own_part(group, k):
+        return lown[at(group * tile, GV, GV), k * planes:(k + 1) * planes].astype(jnp.float32)
+
+    def own_right(group, base):
+        def store(p, k, value):
+            rown[base + p * GV:base + (p + 1) * GV, k * planes:(k + 1) * planes] = value
+        phased(lambda k: own_part(group, k), 0, store)
+
+    def times(a, b):
+        return lax.dot_general(a, b, (((1,), (1,)), ((), ())), preferred_element_type=jnp.float32)
+
+    def finish(group, value):
+        value = value * scale
+        fin[group] = value.reshape(ng, 2, per, rows, 128)
+        for j in range(1, nta):
+            rows_copy(group, lax.rem(t + j, nta)).start()
+        recv[group, t] = fin[group, t // per, :, lax.rem(t, per)]
+
+    lane = lax.broadcasted_iota(jnp.int32, (nta * rows, 128), 1) // GV
+
+    def assemble(b):
+        parts = []
+        for g in range(ng):
+            arrived = recv.at[b * ng + g, pl.ds(0, nta - 1)]
+            pltpu.make_async_copy(arrived, arrived, xrecv.at[b * ng + g]).wait()
+        for c in range(2):
+            for g in range(ng):
+                parts.append(recv[b * ng + g, :, c].reshape(nta * rows, 128))
+        d = moms // 2
+        while d:
+            keep = (lane // d) % 2 == 0
+            later = list(parts)
+            for i in range(moms):
+                if (i // d) % 2 == 0:
+                    low, high = parts[i], parts[i + d]
+                    later[i] = jnp.where(keep, low, pltpu.roll(high, d * GV, 1))
+                    later[i + d] = jnp.where(keep, pltpu.roll(low, 128 - d * GV, 1), high)
+            parts = later
+            d //= 2
+        for p in range(moms):
+            for source in range(nta):
+                out_ref[p, b, :, source, :] = parts[p][source * rows:(source + 1) * rows]
+
+    def norms():
+        squares = []
+        for b in range(NBLK):
+            total = jnp.zeros((BS, 128), jnp.float32)
+            for k in range(2 * NC):
+                for at_lane in range(0, planes, 128):
+                    value = ev_ref[k, b, :, at_lane:at_lane + 128].astype(jnp.float32)
+                    total = total + value * value
+            squares.append(total)
+        nbuf[z] = lax.dot_general(
+            jnp.ones((8, 128), jnp.float32), jnp.concatenate(squares, axis=0), (((1,), (1,)), ((), ())),
+            precision=lax.Precision.HIGHEST, preferred_element_type=jnp.float32,
+        )
+        for j in range(1, n):
+            norm_copy(lax.rem(z + j, n), z).start()
+
+    for b in range(NBLK):
+        stored = order_ref[b]
+        for k in range(2 * NC):
+            value = ev_ref[k, stored]
+            mirror = (k + NC) % (2 * NC)
+            turned = value if k < NC else -value
+            for g in range(ng):
+                base = (b * ng + g) * tile
+                lown[base:base + GV, k * planes:(k + 1) * planes] = value[g * GV:(g + 1) * GV]
+                lown[base + GV:base + tile, mirror * planes:(mirror + 1) * planes] = turned[g * GV:(g + 1) * GV]
+
+    @pl.when(lax.rem(z, n - 1) == 0)
+    def _():
+        def widen(s, group):
+            vsend[s] = lown[at(group * tile, GV, GV), :].astype(jnp.float32)
+
+        def widen_first(s, carry):
+            widen(s, first(s, hi))
+            return carry
+
+        def widen_second(s, carry):
+            widen(s, second(s, hi))
+            return carry
+
+        lax.fori_loop(0, first_groups, widen_first, 0)
+        pl.semaphore_wait(barrier, n - 1 + nta - 1)
+        for s in range(first_groups):
+            vector_copy(s).start()
+        lax.fori_loop(first_groups, groups, widen_second, 0)
+        for s in range(first_groups, groups):
+            vector_copy(s).start()
+        angles(0, z)
+
+        def own(i, carry):
+            for q in range(2):
+                own_right(2 * i + q, q * 128)
+            value = times(lown[at(row0, wide, wide), :], rown[...])
+            for q in range(2):
+                field[2 * i + q, at(row0, wide, wide)] = value[:, q * 128:(q + 1) * 128]
+            return carry
+
+        lax.fori_loop(0, first_groups, own, 0)
+        norms()
+
+        def take(s, group):
+            forward_copy(s, group).wait_recv()
+            finish(group, field[group, at(row0, wide, wide)] + ebuf[group])
+
+        def take_first(s, carry):
+            take(s, first(s, 1 - hi))
+            return carry
+
+        def take_second(s, carry):
+            take(s, second(s, 1 - hi))
+            return carry
+
+        lax.fori_loop(0, first_groups, take_first, 0)
+        lax.fori_loop(first_groups, groups - ng, take_second, 0)
+
+        def put(m, carry):
+            assemble(blk(m, hi))
+            return carry
+
+        lax.fori_loop(0, NBLK - 1, put, 0)
+        lax.fori_loop(groups - ng, groups, take_second, 0)
+        assemble(blk(NBLK - 1, hi))
+
+        def drain(s, carry):
+            vector_copy(s).wait_send()
+            return carry
+
+        lax.fori_loop(0, groups, drain, 0)
+
+    @pl.when(lax.rem(z, n - 1) != 0)
+    def _():
+        angles(0, z)
+        angles(1, end_id)
+
+        def own(i):
+            pair = (first(i, hi), second(i + first_groups, hi))
+            for q in range(2):
+                own_right(pair[q], q * 128)
+            value = times(lown[...], rown[...])
+            for q in range(2):
+                field[pair[q]] = value[:, q * 128:(q + 1) * 128]
+
+        def arrive(s, group):
+            vector_copy(s).wait_recv()
+            base = group * tile
+            for k in range(2 * NC):
+                value = vrecv[s, :, k * planes:(k + 1) * planes]
+                mirror = (k + NC) % (2 * NC)
+                turned = value if k < NC else -value
+                lend[at(base, GV, GV), k * planes:(k + 1) * planes] = value.astype(jnp.bfloat16)
+                lend[at(base + GV, GV, GV), mirror * planes:(mirror + 1) * planes] = turned.astype(jnp.bfloat16)
+
+            def store(p, k, value):
+                rend[s, p * GV:(p + 1) * GV, k * planes:(k + 1) * planes] = value
+            phased(lambda k: vrecv[s, :, k * planes:(k + 1) * planes], 1, store)
+
+        def first_step(s, carry):
+            own(s)
+
+            @pl.when(s == 0)
+            def _():
+                pl.semaphore_wait(barrier, n - 1 + nta - 1)
+                norms()
+
+            group = first(s, hi)
+            arrive(s, group)
+            value = times(lend[at(far, 2 * wide, 2 * wide), :], rend[s])
+            for u in range(2 * ng):
+                came = 2 * (u % ng) + (1 - u // ng) + hi * (2 * (u // ng) - 1)
+
+                @pl.when(came <= s)
+                def _():
+                    field[group, at(far + u * tile, tile, tile)] += value[u * tile:(u + 1) * tile]
+                    tile_copy(s, group, u * tile).start()
+
+            row = group * tile
+            rel = row - far
+
+            def earlier(i, carry):
+                before = first(i, hi)
+                field[before, at(row, tile, tile)] += times(lend[at(row, tile, tile), :], rend[i])
+                tile_copy(i, before, rel).start()
+                return carry
+
+            lax.fori_loop(0, s, earlier, 0)
+            return carry
+
+        lax.fori_loop(0, first_groups, first_step, 0)
+
+        def far_rows(s):
+            group = second(s, hi)
+            arrive(s, group)
+            field[group, at(far, 2 * wide, 2 * wide)] += times(lend[at(far, 2 * wide, 2 * wide), :], rend[s])
+            a_copy(s, group, row3, rel3).start()
+
+            @pl.when(s >= first_groups + 2)
+            def _():
+                b_copy(s - 2, second(s - 2, hi), row2, rel2).start()
+
+        def pass_on(slot, group):
+            field[group, at(row0, wide, wide)] += rbuf[group, at(got0, wide, wide)]
+            forward_copy(slot, group).start()
+
+        def take_a(s):
+            group = second(s, 1 - hi)
+            a_copy(s, group, row0, got0).wait_recv()
+            pass_on(s, group)
+
+        def take_b(s):
+            group = second(s, 1 - hi)
+            b_copy(s, group, row1, got1).wait_recv()
+            field[group, at(row1, wide, wide)] += rbuf[group, at(got1, wide, wide)]
+            finish(group, field[group, at(row1, wide, wide)])
+
+        def take_first(s, carry):
+            group = first(s, 1 - hi)
+            arrived = rbuf.at[group]
+            pltpu.make_async_copy(arrived, arrived, mrecv.at[s]).wait()
+            pass_on(s, group)
+            field[group, at(row1, wide, wide)] += rbuf[group, at(got1, wide, wide)]
+            return carry
+
+        def second_step(s, carry):
+            @pl.when(s == first_groups + 3)
+            def _():
+                lax.fori_loop(0, first_groups, take_first, 0)
+                take_a(first_groups)
+
+            far_rows(s)
+            return carry
+
+        lax.fori_loop(first_groups, groups - ng, second_step, 0)
+
+        def third_step(s, carry):
+            step = s - (groups - ng)
+            take_a(s - 3)
+
+            @pl.when(step >= 1)
+            def _():
+                take_b(s - 5)
+
+            far_rows(s)
+            group = second(s, hi)
+            near = lend[at(row1, wide, wide), :]
+            finish(group, field[group, at(row1, wide, wide)] + times(near, rend[s]))
+
+            @pl.when(step < ng - 1)
+            def _():
+                late = step // 2
+
+                def catch_up(q, carry):
+                    odd = 2 * q + 1 - lax.rem(step, 2)
+                    slot = late * (first_groups + q) + (1 - late) * odd
+                    before = late * second(first_groups + q, hi) + (1 - late) * first(odd, hi)
+                    field[before, at(row1, wide, wide)] += times(lend[at(row1, wide, wide), :], rend[slot])
+
+                    @pl.when(late == 1)
+                    def _():
+                        finish(before, field[before, at(row1, wide, wide)])
+                    return carry
+
+                lax.fori_loop(0, ng, catch_up, 0)
+            return carry
+
+        lax.fori_loop(groups - ng, groups, third_step, 0)
+        for s in (groups - 2, groups - 1):
+            b_copy(s, second(s, hi), row2, rel2).start()
+
+        def last_a(s, carry):
+            take_a(s)
+            return carry
+
+        def last_b(s, carry):
+            take_b(s)
+            return carry
+
+        lax.fori_loop(groups - 3, groups - 1, last_a, 0)
+        lax.fori_loop(groups - 5, groups - ng, last_b, 0)
+        lax.fori_loop(groups - 1, groups, last_a, 0)
+
+        def put(m, carry):
+            assemble(blk(m, hi))
+            return carry
+
+        lax.fori_loop(0, NBLK - 1, put, 0)
+        lax.fori_loop(groups - ng, groups, last_b, 0)
+        assemble(blk(NBLK - 1, hi))
+
+        def drain(s, carry):
+            sent = rbuf.at[s]
+            pltpu.make_async_copy(sent, sent, msend.at[s]).wait()
+            forward_copy(s, s).wait_send()
+            return carry
+
+        lax.fori_loop(0, groups, drain, 0)
+
+    for j in range(1, n):
+        norm_copy(lax.rem(z + j, n), lax.rem(z + j, n)).wait_recv()
+    total = nbuf[0]
+    for q in range(1, n):
+        total = total + nbuf[q]
+    norm_ref[...] = total[0:1] * inv_count
+    for j in range(1, n):
+        norm_copy(lax.rem(z + j, n), z).wait_send()
+
+    def drain_rows(group, carry):
+        sent = recv.at[group, pl.ds(0, nta - 1)]
+        pltpu.make_async_copy(sent, sent, xsend.at[group]).wait()
+        return carry
+
+    lax.fori_loop(0, groups, drain_rows, 0)
+
+
+def pair_scratch(n, nta, moms, nv, planes):
+    f32, bf16 = jnp.float32, jnp.bfloat16
+    deep = 2 * NC * planes
+    ng = BS // GV
+    groups = NBLK * ng
+    rows = BS // nta
+    dma = pltpu.SemaphoreType.DMA
+    return [
+        pltpu.VMEM((2 * nv, deep), bf16),
+        pltpu.VMEM((2 * nv, deep), bf16),
+        pltpu.VMEM((256, deep), bf16),
+        pltpu.VMEM((groups, moms * GV, deep), bf16),
+        pltpu.VMEM((2, 2, moms, planes), f32),
+        pltpu.VMEM((groups, GV, deep), f32),
+        pltpu.VMEM((groups, GV, deep), f32),
+        pltpu.VMEM((groups, 2 * nv, 128), f32),
+        pltpu.VMEM((groups, nv, 128), f32),
+        pltpu.VMEM((groups, 2 * BS, 128), f32),
+        pltpu.VMEM((groups, ng, 2, GV // rows, rows, 128), f32),
+        pltpu.VMEM((groups, nta, 2, rows, 128), f32),
+        pltpu.VMEM((n, 8, nv), f32),
+        dma((groups,)), dma((groups,)), dma((groups,)), dma((groups // 2,)),
+        dma((groups // 2,)), dma((groups // 2,)), dma((groups,)), dma((groups,)),
+        dma((groups,)), dma((groups,)), dma((n,)), dma((n,)),
+    ]
+
+
+def line_scratch(n, nta, moms, nv, planes):
+    f32 = jnp.float32
+    ppd = NBLK * NBLK // n
+    rows = BS // nta
+    dma = pltpu.SemaphoreType.DMA
+    return [
+        pltpu.VMEM((nv, 2 * NC * planes), jnp.bfloat16),
+        pltpu.VMEM((2 * nv, 2 * NC * planes), jnp.bfloat16),
+        pltpu.VMEM((moms, NBLK * NBLK, BS, 2 * BS), f32),
+        pltpu.VMEM((moms, NBLK * NBLK, BS, 2 * BS), f32),
+        pltpu.VMEM((moms, NBLK * NBLK, BS, 2 * BS), f32),
+        pltpu.VMEM((moms, nta, ppd, rows, 2 * BS), f32),
+        pltpu.VMEM((moms, nta, ppd, rows, 2 * BS), f32),
+        pltpu.VMEM((n, 8, nv), f32),
+        dma((moms, n)), dma((moms, n)), dma((moms, n)), dma((moms, n)),
+        dma((moms,)), dma((moms,)), dma((n,)), dma((n,)),
+    ]
+
+
 def body(eigenvectors, momenta, block_order):
     planes = eigenvectors.shape[-1]
     n, nta = lax.axis_size("sa"), lax.axis_size("ta")
@@ -246,7 +718,8 @@
     f32 = jnp.float32
     vmem = pl.BlockSpec(memory_space=pltpu.VMEM)
     smem = pl.BlockSpec(memory_space=pltpu.SMEM)
-    dma = pltpu.SemaphoreType.DMA
+    paired = n == NBLK == 4 and moms * GV == 128 and rows % 8 == 0 and GV % rows == 0
+    kernel, scratch = (pair_kernel, pair_scratch) if paired else (line_kernel, line_scratch)
     fields, norms = pl.pallas_call(
         functools.partial(kernel, n, nta, 1.0 / math.sqrt(count), 1.0 / count),
         out_shape=(
@@ -255,19 +728,8 @@
         ),
         in_specs=[smem, smem, vmem],
         out_specs=(vmem, vmem),
-        scratch_shapes=[
-            pltpu.VMEM((nv, 2 * NC * planes), jnp.bfloat16),
-            pltpu.VMEM((2 * nv, 2 * NC * planes), jnp.bfloat16),
-            pltpu.VMEM((moms, NBLK * NBLK, BS, 2 * BS), f32),
-            pltpu.VMEM((moms, NBLK * NBLK, BS, 2 * BS), f32),
-            pltpu.VMEM((moms, NBLK * NBLK, BS, 2 * BS), f32),
-            pltpu.VMEM((moms, nta, ppd, rows, 2 * BS), f32),
-            pltpu.VMEM((moms, nta, ppd, rows, 2 * BS), f32),
-            pltpu.VMEM((n, 8, nv), f32),
-            dma((moms, n)), dma((moms, n)), dma((moms, n)), dma((moms, n)),
-            dma((moms,)), dma((moms,)), dma((n,)), dma((n,)),
-        ],
-        compiler_params=pltpu.CompilerParams(collective_id=0, has_side_effects=True, vmem_limit_bytes=30 * 1024 * 1024),
+        scratch_shapes=scratch(n, nta, moms, nv, planes),
+        compiler_params=pltpu.CompilerParams(collective_id=0, has_side_effects=True, vmem_limit_bytes=48 * 1024 * 1024),
     )(block_order, momenta.T, stored)
     return fields, norms
 

time: 83.6 us -> 77 us (0.921)
  Pallas kernels: 79.8 us -> 73.2 us
    pallas_call x1, Pallas kernels: 79.8 us -> 73.2 us  [body(): pl.pallas_call(functools.partial(kernel, n, nta, 1.0 / math.sqrt(count),...]
where the time goes in v1:
time: 77 us; the launch traced here: 76.9 us
  Pallas kernels  73.2 us (95%)
  local copies, waits for them, and re-layouts  2.98 us (4%)
    pallas_call x1, Pallas kernels, body(): pl.pallas_call(functools.partial(kernel, n, nta, 1.0 / math.sqrt(count),...  73.2 us
    unnamed x7, local copies, waits for them, and re-layouts  2.98 us

profile of v1, /device:TPU:0, one launch (start us, length us, event | category | flops | bytes accessed | tf_op | source)
XLA Modules:
  0.0 76.9 jit_solution(9251480103872824604)
XLA Ops:
  0.6 0.0 copy-start
  0.6 0.0 copy-start.1
  0.6 1.4 %copy.5 = bf16[1,256,2,3,1,384]{5,1,3,2,4,0:T(8,128)(2,1)S(1)} copy(bf16[1,256,2,3,1,384]{5,2,4,3,1,0:T(2,128)(2,1)} %param.3) | data formatting | bytes 2359296 | tf_op args[0]
  2.1 0.0 copy-done
  2.1 0.0 copy-done.1
  2.1 73.2 %shard_map.50 = (f32[8,4,8,8,128]{4,3,2,1,0:T(8,128)S(1)}, f32[1,256]{1,0:T(1,128)S(1)}) custom-call(s32[4]{0:T(128)S(1)} %copy-done.1, s32[3,8]{1,0:T(4,128)S(1)} %bitcast.5, bf16[6,4,64,384]{3,2,1,0:T(8,128)(2,1)S(1)} %bitcast.4), custom_call_target="tpu_custom_call" | custom-call | tf_op jit(solution)/shard_map/pallas_call | solution.py:723
  75.3 1.0 %copy.8 = f32[8,4,8,8,128]{4,3,2,1,0:T(8,128)} copy(f32[8,4,8,8,128]{4,3,2,1,0:T(8,128)S(1)} %get-tuple-element.4) | data formatting | bytes 2097152
  76.3 0.6 copy.9
Async XLA Ops:
  0.6 1.5 %copy-start = (s32[8,3]{0,1:T(4,128)S(1)}, s32[8,3]{0,1:T(4,128)}, u32[]{:S(2)}) copy-start(s32[8,3]{0,1:T(4,128)} %param.4) | copy-start | bytes 292
  0.6 1.5 %copy-start.1 = (s32[4]{0:T(128)S(1)}, s32[4]{0:T(128)}, u32[]{:S(2)}) copy-start(s32[4]{0:T(128)} %order_ref.1) | copy-start | bytes 52

commit v2 on v1

--- a/solution.py
+++ b/solution.py
@@ -241,8 +241,8 @@
     n, nta, scale, inv_count,
     order_ref, momenta_ref, ev_ref,
     out_ref, norm_ref,
-    lown, lend, rown, rend, trig, vsend, vrecv, field, rbuf, ebuf, fin, recv, nbuf,
-    vss, vrs, msend, mrecv, arecv, brecv, fsend, frecv, xsend, xrecv, nsend, nrecv,
+    lown, lend, rown, rend, trig, vsend, vrecv, field, rbuf, ebuf, fin, recv, straight, late, nbuf,
+    vss, vrs, msend, mrecv, arecv, brecv, fsend, frecv, xsend, xrecv, lsend, lrecv, nsend, nrecv, ready,
 ):
     t, z = lax.axis_index("ta"), lax.axis_index("sa")
     moms, planes = momenta_ref.shape[1], ev_ref.shape[-1]
@@ -279,10 +279,18 @@
     got0, got1 = hi * wide, (1 - hi) * wide
 
     barrier = pltpu.get_barrier_semaphore()
-    for j in range(1, n):
-        pl.semaphore_signal(barrier, inc=1, device_id={"sa": lax.rem(z + j, n)}, device_id_type=MESH)
-    for j in range(1, nta):
-        pl.semaphore_signal(barrier, inc=1, device_id={"ta": lax.rem(t + j, nta)}, device_id_type=MESH)
+    is_end = lax.rem(z, n - 1) == 0
+
+    @pl.when(is_end)
+    def _():
+        pl.semaphore_signal(barrier, inc=1, device_id={"sa": mid_id}, device_id_type=MESH)
+
+    @pl.when(jnp.logical_not(is_end))
+    def _():
+        for peer in (end_id, other_id):
+            pl.semaphore_signal(barrier, inc=1, device_id={"sa": peer}, device_id_type=MESH)
+        for j in range(1, nta):
+            pl.semaphore_signal(barrier, inc=1, device_id={"ta": lax.rem(t + j, nta)}, device_id_type=MESH)
 
     def remote(src, dst, send_sem, recv_sem, peer):
         return pltpu.make_async_remote_copy(
@@ -314,8 +322,15 @@
     def forward_copy(slot, group):
         return remote(field.at[group, at(row0, wide, wide)], ebuf.at[group], fsend.at[slot], frecv.at[slot], end_id)
 
-    def norm_copy(peer, slot):
-        return remote(nbuf.at[slot], nbuf.at[slot], nsend.at[peer], nrecv.at[slot], peer)
+    def norm_copy(i, peer):
+        return remote(nbuf.at[2 * i], nbuf.at[2 * i + 1], nsend.at[i], nrecv.at[i], peer)
+
+    def straight_copy(i, part, row_peer, peer):
+        return pltpu.make_async_remote_copy(
+            src_ref=straight.at[i, part, row_peer // per, :, lax.rem(row_peer, per)], dst_ref=late.at[i, t],
+            send_sem=lsend.at[i], recv_sem=lrecv.at[i],
+            device_id={"ta": row_peer, "sa": peer}, device_id_type=MESH,
+        )
 
     def rows_copy(group, peer):
         return pltpu.make_async_remote_copy(
@@ -364,14 +379,19 @@
 
     lane = lax.broadcasted_iota(jnp.int32, (nta * rows, 128), 1) // GV
 
-    def assemble(b):
+    def assemble(b, last):
         parts = []
         for g in range(ng):
             arrived = recv.at[b * ng + g, pl.ds(0, nta - 1)]
             pltpu.make_async_copy(arrived, arrived, xrecv.at[b * ng + g]).wait()
+            if last:
+                pltpu.make_async_copy(late.at[g], late.at[g], lrecv.at[g]).wait()
         for c in range(2):
             for g in range(ng):
-                parts.append(recv[b * ng + g, :, c].reshape(nta * rows, 128))
+                part = recv[b * ng + g, :, c].reshape(nta * rows, 128)
+                if last:
+                    part = part + late[g, :, c].reshape(nta * rows, 128)
+                parts.append(part)
         d = moms // 2
         while d:
             keep = (lane // d) % 2 == 0
@@ -396,12 +416,10 @@
                     value = ev_ref[k, b, :, at_lane:at_lane + 128].astype(jnp.float32)
                     total = total + value * value
             squares.append(total)
-        nbuf[z] = lax.dot_general(
+        nbuf[0] = lax.dot_general(
             jnp.ones((8, 128), jnp.float32), jnp.concatenate(squares, axis=0), (((1,), (1,)), ((), ())),
             precision=lax.Precision.HIGHEST, preferred_element_type=jnp.float32,
         )
-        for j in range(1, n):
-            norm_copy(lax.rem(z + j, n), z).start()
 
     for b in range(NBLK):
         stored = order_ref[b]
@@ -414,7 +432,7 @@
                 lown[base:base + GV, k * planes:(k + 1) * planes] = value[g * GV:(g + 1) * GV]
                 lown[base + GV:base + tile, mirror * planes:(mirror + 1) * planes] = turned[g * GV:(g + 1) * GV]
 
-    @pl.when(lax.rem(z, n - 1) == 0)
+    @pl.when(is_end)
     def _():
         def widen(s, group):
             vsend[s] = lown[at(group * tile, GV, GV), :].astype(jnp.float32)
@@ -428,8 +446,12 @@
             return carry
 
         lax.fori_loop(0, first_groups, widen_first, 0)
-        pl.semaphore_wait(barrier, n - 1 + nta - 1)
-        for s in range(first_groups):
+        pl.semaphore_wait(barrier, 1)
+        for s in range(ng):
+            vector_copy(s).start()
+        norms()
+        norm_copy(0, mid_id).start()
+        for s in range(ng, first_groups):
             vector_copy(s).start()
         lax.fori_loop(first_groups, groups, widen_second, 0)
         for s in range(first_groups, groups):
@@ -445,7 +467,6 @@
             return carry
 
         lax.fori_loop(0, first_groups, own, 0)
-        norms()
 
         def take(s, group):
             forward_copy(s, group).wait_recv()
@@ -460,15 +481,19 @@
             return carry
 
         lax.fori_loop(0, first_groups, take_first, 0)
+        lax.fori_loop(groups - ng, groups, take_second, 0)
+
+        def put(m, carry):
+            assemble(blk(m, hi), False)
+            return carry
+
+        lax.fori_loop(0, 2, put, 0)
         lax.fori_loop(first_groups, groups - ng, take_second, 0)
-
-        def put(m, carry):
-            assemble(blk(m, hi))
-            return carry
-
-        lax.fori_loop(0, NBLK - 1, put, 0)
-        lax.fori_loop(groups - ng, groups, take_second, 0)
-        assemble(blk(NBLK - 1, hi))
+        lax.fori_loop(2, NBLK - 1, put, 0)
+        norm_copy(2, end_id).wait_recv()
+        norm_ref[...] = nbuf[5, 0:1] * inv_count
+        assemble(blk(NBLK - 1, hi), True)
+        norm_copy(0, mid_id).wait_send()
 
         def drain(s, carry):
             vector_copy(s).wait_send()
@@ -476,7 +501,7 @@
 
         lax.fori_loop(0, groups, drain, 0)
 
-    @pl.when(lax.rem(z, n - 1) != 0)
+    @pl.when(jnp.logical_not(is_end))
     def _():
         angles(0, z)
         angles(1, end_id)
@@ -508,10 +533,18 @@
 
             @pl.when(s == 0)
             def _():
-                pl.semaphore_wait(barrier, n - 1 + nta - 1)
+                pl.semaphore_wait(barrier, nta + 1)
+                for j in range(1, nta):
+                    pl.semaphore_signal(ready, inc=1, device_id={"ta": lax.rem(t + j, nta)}, device_id_type=MESH)
                 norms()
+                pl.semaphore_wait(ready, nta - 1)
 
             group = first(s, hi)
+
+            @pl.when(lax.rem(s, 2) == 0)
+            def _():
+                forward_copy(groups - ng + s // 2, group).start()
+
             arrive(s, group)
             value = times(lend[at(far, 2 * wide, 2 * wide), :], rend[s])
             for u in range(2 * ng):
@@ -540,11 +573,22 @@
             group = second(s, hi)
             arrive(s, group)
             field[group, at(far, 2 * wide, 2 * wide)] += times(lend[at(far, 2 * wide, 2 * wide), :], rend[s])
-            a_copy(s, group, row3, rel3).start()
-
-            @pl.when(s >= first_groups + 2)
-            def _():
-                b_copy(s - 2, second(s - 2, hi), row2, rel2).start()
+            return group
+
+        def send_b(s):
+            b_copy(s, second(s, hi), row2, rel2).start()
+
+        def send_straight(i, part, group, row, peer):
+            value = field[group, at(row, wide, wide)] * scale
+            straight[i, part] = value.reshape(ng, 2, per, rows, 128)
+            for j in range(nta):
+                straight_copy(i, part, lax.rem(t + j, nta), peer).start()
+
+        def straight_a(s):
+            send_straight(s - (groups - ng), 0, second(s, hi), row3, n - 1 - end_id)
+
+        def straight_b(s):
+            send_straight(s - (groups - ng), 1, second(s, hi), row2, other_id)
 
         def pass_on(slot, group):
             field[group, at(row0, wide, wide)] += rbuf[group, at(got0, wide, wide)]
@@ -569,41 +613,78 @@
             field[group, at(row1, wide, wide)] += rbuf[group, at(got1, wide, wide)]
             return carry
 
+        def last_a(s, carry):
+            take_a(s)
+            return carry
+
         def second_step(s, carry):
+            @pl.when(s == first_groups + 2)
+            def _():
+                lax.fori_loop(0, first_groups, take_first, 0)
+
             @pl.when(s == first_groups + 3)
             def _():
-                lax.fori_loop(0, first_groups, take_first, 0)
-                take_a(first_groups)
-
-            far_rows(s)
+                lax.fori_loop(first_groups, first_groups + 2, last_a, 0)
+
+            @pl.when(s == first_groups)
+            def _():
+                norm_copy(0, mid_id).wait_recv()
+                nbuf[2] = nbuf[0] + nbuf[1]
+                norm_copy(1, other_id).start()
+
+            group = far_rows(s)
+            a_copy(s, group, row3, rel3).start()
+
+            @pl.when(s >= first_groups + 2)
+            def _():
+                send_b(s - 2)
             return carry
 
         lax.fori_loop(first_groups, groups - ng, second_step, 0)
 
         def third_step(s, carry):
             step = s - (groups - ng)
-            take_a(s - 3)
-
-            @pl.when(step >= 1)
-            def _():
-                take_b(s - 5)
-
-            far_rows(s)
-            group = second(s, hi)
+
+            @pl.when(step == 0)
+            def _():
+                norm_copy(1, other_id).wait_recv()
+                total = nbuf[2] + nbuf[3]
+                nbuf[4] = total
+                norm_ref[...] = total[0:1] * inv_count
+                norm_copy(2, end_id).start()
+
+            @pl.when(step < 2)
+            def _():
+                take_a(s - 2)
+
+            @pl.when(step >= 2)
+            def _():
+                take_b(s - 6)
+
+            group = far_rows(s)
+            straight_a(s)
+
+            @pl.when(step < 2)
+            def _():
+                send_b(s - 2)
+
+            @pl.when(step >= 2)
+            def _():
+                straight_b(s - 2)
             near = lend[at(row1, wide, wide), :]
             finish(group, field[group, at(row1, wide, wide)] + times(near, rend[s]))
 
             @pl.when(step < ng - 1)
             def _():
-                late = step // 2
+                later = (2 - step) // 2
 
                 def catch_up(q, carry):
-                    odd = 2 * q + 1 - lax.rem(step, 2)
-                    slot = late * (first_groups + q) + (1 - late) * odd
-                    before = late * second(first_groups + q, hi) + (1 - late) * first(odd, hi)
+                    odd = 2 * q + 2 - step
+                    slot = later * (first_groups + q) + (1 - later) * odd
+                    before = later * second(first_groups + q, hi) + (1 - later) * first(odd, hi)
                     field[before, at(row1, wide, wide)] += times(lend[at(row1, wide, wide), :], rend[slot])
 
-                    @pl.when(late == 1)
+                    @pl.when(step != 1)
                     def _():
                         finish(before, field[before, at(row1, wide, wide)])
                     return carry
@@ -612,45 +693,37 @@
             return carry
 
         lax.fori_loop(groups - ng, groups, third_step, 0)
-        for s in (groups - 2, groups - 1):
-            b_copy(s, second(s, hi), row2, rel2).start()
-
-        def last_a(s, carry):
-            take_a(s)
-            return carry
-
-        def last_b(s, carry):
-            take_b(s)
-            return carry
-
-        lax.fori_loop(groups - 3, groups - 1, last_a, 0)
-        lax.fori_loop(groups - 5, groups - ng, last_b, 0)
-        lax.fori_loop(groups - 1, groups, last_a, 0)
+        straight_b(groups - 2)
+        straight_b(groups - 1)
+        take_b(groups - 6)
+        take_b(groups - 5)
 
         def put(m, carry):
-            assemble(blk(m, hi))
+            assemble(blk(m, hi), False)
             return carry
 
         lax.fori_loop(0, NBLK - 1, put, 0)
-        lax.fori_loop(groups - ng, groups, last_b, 0)
-        assemble(blk(NBLK - 1, hi))
+        assemble(blk(NBLK - 1, hi), True)
+        norm_copy(1, other_id).wait_send()
+        norm_copy(2, end_id).wait_send()
 
         def drain(s, carry):
+            forward_copy(s, s).wait_send()
+            return carry
+
+        def drain_sums(s, carry):
             sent = rbuf.at[s]
             pltpu.make_async_copy(sent, sent, msend.at[s]).wait()
-            forward_copy(s, s).wait_send()
+            return carry
+
+        def drain_straight(i, carry):
+            sent = straight.at[i]
+            pltpu.make_async_copy(sent, sent, lsend.at[i]).wait()
             return carry
 
         lax.fori_loop(0, groups, drain, 0)
-
-    for j in range(1, n):
-        norm_copy(lax.rem(z + j, n), lax.rem(z + j, n)).wait_recv()
-    total = nbuf[0]
-    for q in range(1, n):
-        total = total + nbuf[q]
-    norm_ref[...] = total[0:1] * inv_count
-    for j in range(1, n):
-        norm_copy(lax.rem(z + j, n), z).wait_send()
+        lax.fori_loop(0, groups - ng, drain_sums, 0)
+        lax.fori_loop(0, ng, drain_straight, 0)
 
     def drain_rows(group, carry):
         sent = recv.at[group, pl.ds(0, nta - 1)]
@@ -680,10 +753,13 @@
         pltpu.VMEM((groups, 2 * BS, 128), f32),
         pltpu.VMEM((groups, ng, 2, GV // rows, rows, 128), f32),
         pltpu.VMEM((groups, nta, 2, rows, 128), f32),
-        pltpu.VMEM((n, 8, nv), f32),
+        pltpu.VMEM((ng, 2, ng, 2, GV // rows, rows, 128), f32),
+        pltpu.VMEM((ng, nta, 2, rows, 128), f32),
+        pltpu.VMEM((6, 8, nv), f32),
         dma((groups,)), dma((groups,)), dma((groups,)), dma((groups // 2,)),
         dma((groups // 2,)), dma((groups // 2,)), dma((groups,)), dma((groups,)),
-        dma((groups,)), dma((groups,)), dma((n,)), dma((n,)),
+        dma((groups,)), dma((groups,)), dma((ng,)), dma((ng,)), dma((3,)), dma((3,)),
+        pltpu.SemaphoreType.REGULAR,
     ]
 
 

time: 77 us -> 72.8 us (0.945)
  Pallas kernels: 73.2 us -> 69 us
    pallas_call x1, Pallas kernels: 73.2 us -> 69 us  [body(): pl.pallas_call(functools.partial(kernel, n, nta, 1.0 / math.sqrt(count),...]
where the time goes in v2:
time: 72.8 us; the launch traced here: 72.6 us
  Pallas kernels  69 us (95%)
  local copies, waits for them, and re-layouts  2.98 us (4%)
    pallas_call x1, Pallas kernels, body(): pl.pallas_call(functools.partial(kernel, n, nta, 1.0 / math.sqrt(count),...  69 us
    unnamed x7, local copies, waits for them, and re-layouts  2.98 us

profile of v2, /device:TPU:0, one launch (start us, length us, event | category | flops | bytes accessed | tf_op | source)
XLA Modules:
  0.0 72.6 jit_solution(7814425930625370243)
XLA Ops:
  0.6 0.0 copy-start
  0.6 0.0 copy-start.1
  0.6 1.4 %copy.5 = bf16[1,256,2,3,1,384]{5,1,3,2,4,0:T(8,128)(2,1)S(1)} copy(bf16[1,256,2,3,1,384]{5,2,4,3,1,0:T(2,128)(2,1)} %param.3) | data formatting | bytes 2359296 | tf_op args[0]
  2.1 0.0 copy-done
  2.1 0.0 copy-done.1
  2.1 69.0 %shard_map.50 = (f32[8,4,8,8,128]{4,3,2,1,0:T(8,128)S(1)}, f32[1,256]{1,0:T(1,128)S(1)}) custom-call(s32[4]{0:T(128)S(1)} %copy-done.1, s32[3,8]{1,0:T(4,128)S(1)} %bitcast.5, bf16[6,4,64,384]{3,2,1,0:T(8,128)(2,1)S(1)} %bitcast.4), custom_call_target="tpu_custom_call" | custom-call | tf_op jit(solution)/shard_map/pallas_call | solution.py:799
  71.1 1.0 %copy.8 = f32[8,4,8,8,128]{4,3,2,1,0:T(8,128)} copy(f32[8,4,8,8,128]{4,3,2,1,0:T(8,128)S(1)} %get-tuple-element.4) | data formatting | bytes 2097152
  72.1 0.6 copy.9
Async XLA Ops:
  0.6 1.5 %copy-start = (s32[8,3]{0,1:T(4,128)S(1)}, s32[8,3]{0,1:T(4,128)}, u32[]{:S(2)}) copy-start(s32[8,3]{0,1:T(4,128)} %param.4) | copy-start | bytes 292
  0.6 1.5 %copy-start.1 = (s32[4]{0:T(128)S(1)}, s32[4]{0:T(128)}, u32[]{:S(2)}) copy-start(s32[4]{0:T(128)} %order_ref.1) | copy-start | bytes 52

commit v3 on v2

--- a/solution.py
+++ b/solution.py
@@ -327,14 +327,14 @@
 
     def straight_copy(i, part, row_peer, peer):
         return pltpu.make_async_remote_copy(
-            src_ref=straight.at[i, part, row_peer // per, :, lax.rem(row_peer, per)], dst_ref=late.at[i, t],
+            src_ref=straight.at[i, part, row_peer], dst_ref=late.at[i, t],
             send_sem=lsend.at[i], recv_sem=lrecv.at[i],
             device_id={"ta": row_peer, "sa": peer}, device_id_type=MESH,
         )
 
     def rows_copy(group, peer):
         return pltpu.make_async_remote_copy(
-            src_ref=fin.at[group, peer // per, :, lax.rem(peer, per)], dst_ref=recv.at[group, t],
+            src_ref=fin.at[group, peer], dst_ref=recv.at[group, t],
             send_sem=xsend.at[group], recv_sem=xrecv.at[group],
             device_id={"ta": peer}, device_id_type=MESH,
         )
@@ -370,12 +370,17 @@
     def times(a, b):
         return lax.dot_general(a, b, (((1,), (1,)), ((), ())), preferred_element_type=jnp.float32)
 
+    def split(value, ref):
+        for peer in range(nta):
+            for c in range(2):
+                base = peer // per * tile + c * GV + peer % per * rows
+                ref[peer, c] = value[base:base + rows]
+
     def finish(group, value):
-        value = value * scale
-        fin[group] = value.reshape(ng, 2, per, rows, 128)
+        split(value * scale, fin.at[group])
         for j in range(1, nta):
             rows_copy(group, lax.rem(t + j, nta)).start()
-        recv[group, t] = fin[group, t // per, :, lax.rem(t, per)]
+        recv[group, t] = fin[group, t]
 
     lane = lax.broadcasted_iota(jnp.int32, (nta * rows, 128), 1) // GV
 
@@ -407,6 +412,11 @@
             for source in range(nta):
                 out_ref[p, b, :, source, :] = parts[p][source * rows:(source + 1) * rows]
 
+    def drain_rows(group, carry):
+        sent = recv.at[group, pl.ds(0, nta - 1)]
+        pltpu.make_async_copy(sent, sent, xsend.at[group]).wait()
+        return carry
+
     def norms():
         squares = []
         for b in range(NBLK):
@@ -421,21 +431,25 @@
             precision=lax.Precision.HIGHEST, preferred_element_type=jnp.float32,
         )
 
-    for b in range(NBLK):
-        stored = order_ref[b]
-        for k in range(2 * NC):
-            value = ev_ref[k, stored]
-            mirror = (k + NC) % (2 * NC)
-            turned = value if k < NC else -value
-            for g in range(ng):
-                base = (b * ng + g) * tile
-                lown[base:base + GV, k * planes:(k + 1) * planes] = value[g * GV:(g + 1) * GV]
-                lown[base + GV:base + tile, mirror * planes:(mirror + 1) * planes] = turned[g * GV:(g + 1) * GV]
+    def build():
+        for b in range(NBLK):
+            stored = order_ref[b]
+            for k in range(2 * NC):
+                value = ev_ref[k, stored]
+                mirror = (k + NC) % (2 * NC)
+                turned = value if k < NC else -value
+                for g in range(ng):
+                    base = (b * ng + g) * tile
+                    lown[base:base + GV, k * planes:(k + 1) * planes] = value[g * GV:(g + 1) * GV]
+                    lown[base + GV:base + tile, mirror * planes:(mirror + 1) * planes] = turned[g * GV:(g + 1) * GV]
 
     @pl.when(is_end)
     def _():
         def widen(s, group):
-            vsend[s] = lown[at(group * tile, GV, GV), :].astype(jnp.float32)
+            stored = order_ref[group // ng]
+            for k in range(2 * NC):
+                value = ev_ref[k, stored, at(lax.rem(group, ng) * GV, GV, GV), :]
+                vsend[s, :, k * planes:(k + 1) * planes] = value.astype(jnp.float32)
 
         def widen_first(s, carry):
             widen(s, first(s, hi))
@@ -445,10 +459,11 @@
             widen(s, second(s, hi))
             return carry
 
-        lax.fori_loop(0, first_groups, widen_first, 0)
+        lax.fori_loop(0, ng, widen_first, 0)
         pl.semaphore_wait(barrier, 1)
         for s in range(ng):
             vector_copy(s).start()
+        lax.fori_loop(ng, first_groups, widen_first, 0)
         norms()
         norm_copy(0, mid_id).start()
         for s in range(ng, first_groups):
@@ -457,6 +472,7 @@
         for s in range(first_groups, groups):
             vector_copy(s).start()
         angles(0, z)
+        build()
 
         def own(i, carry):
             for q in range(2):
@@ -492,7 +508,6 @@
         lax.fori_loop(2, NBLK - 1, put, 0)
         norm_copy(2, end_id).wait_recv()
         norm_ref[...] = nbuf[5, 0:1] * inv_count
-        assemble(blk(NBLK - 1, hi), True)
         norm_copy(0, mid_id).wait_send()
 
         def drain(s, carry):
@@ -500,9 +515,12 @@
             return carry
 
         lax.fori_loop(0, groups, drain, 0)
+        lax.fori_loop(0, groups, drain_rows, 0)
+        assemble(blk(NBLK - 1, hi), True)
 
     @pl.when(jnp.logical_not(is_end))
     def _():
+        build()
         angles(0, z)
         angles(1, end_id)
 
@@ -514,10 +532,10 @@
             for q in range(2):
                 field[pair[q]] = value[:, q * 128:(q + 1) * 128]
 
-        def arrive(s, group):
+        def arrive(s, group, rows_too=True):
             vector_copy(s).wait_recv()
             base = group * tile
-            for k in range(2 * NC):
+            for k in range(2 * NC if rows_too else 0):
                 value = vrecv[s, :, k * planes:(k + 1) * planes]
                 mirror = (k + NC) % (2 * NC)
                 turned = value if k < NC else -value
@@ -569,9 +587,9 @@
 
         lax.fori_loop(0, first_groups, first_step, 0)
 
-        def far_rows(s):
+        def far_rows(s, rows_too):
             group = second(s, hi)
-            arrive(s, group)
+            arrive(s, group, rows_too)
             field[group, at(far, 2 * wide, 2 * wide)] += times(lend[at(far, 2 * wide, 2 * wide), :], rend[s])
             return group
 
@@ -579,8 +597,7 @@
             b_copy(s, second(s, hi), row2, rel2).start()
 
         def send_straight(i, part, group, row, peer):
-            value = field[group, at(row, wide, wide)] * scale
-            straight[i, part] = value.reshape(ng, 2, per, rows, 128)
+            split(field[group, at(row, wide, wide)] * scale, straight.at[i, part])
             for j in range(nta):
                 straight_copy(i, part, lax.rem(t + j, nta), peer).start()
 
@@ -632,12 +649,10 @@
                 nbuf[2] = nbuf[0] + nbuf[1]
                 norm_copy(1, other_id).start()
 
-            group = far_rows(s)
+            group = far_rows(s, True)
             a_copy(s, group, row3, rel3).start()
 
-            @pl.when(s >= first_groups + 2)
-            def _():
-                send_b(s - 2)
+            send_b(s)
             return carry
 
         lax.fori_loop(first_groups, groups - ng, second_step, 0)
@@ -661,16 +676,10 @@
             def _():
                 take_b(s - 6)
 
-            group = far_rows(s)
+            group = far_rows(s, False)
             straight_a(s)
 
-            @pl.when(step < 2)
-            def _():
-                send_b(s - 2)
-
-            @pl.when(step >= 2)
-            def _():
-                straight_b(s - 2)
+            straight_b(s)
             near = lend[at(row1, wide, wide), :]
             finish(group, field[group, at(row1, wide, wide)] + times(near, rend[s]))
 
@@ -693,8 +702,6 @@
             return carry
 
         lax.fori_loop(groups - ng, groups, third_step, 0)
-        straight_b(groups - 2)
-        straight_b(groups - 1)
         take_b(groups - 6)
         take_b(groups - 5)
 
@@ -703,7 +710,6 @@
             return carry
 
         lax.fori_loop(0, NBLK - 1, put, 0)
-        assemble(blk(NBLK - 1, hi), True)
         norm_copy(1, other_id).wait_send()
         norm_copy(2, end_id).wait_send()
 
@@ -723,14 +729,9 @@
 
         lax.fori_loop(0, groups, drain, 0)
         lax.fori_loop(0, groups - ng, drain_sums, 0)
+        lax.fori_loop(0, groups, drain_rows, 0)
         lax.fori_loop(0, ng, drain_straight, 0)
-
-    def drain_rows(group, carry):
-        sent = recv.at[group, pl.ds(0, nta - 1)]
-        pltpu.make_async_copy(sent, sent, xsend.at[group]).wait()
-        return carry
-
-    lax.fori_loop(0, groups, drain_rows, 0)
+        assemble(blk(NBLK - 1, hi), True)
 
 
 def pair_scratch(n, nta, moms, nv, planes):
@@ -751,9 +752,9 @@
         pltpu.VMEM((groups, 2 * nv, 128), f32),
         pltpu.VMEM((groups, nv, 128), f32),
         pltpu.VMEM((groups, 2 * BS, 128), f32),
-        pltpu.VMEM((groups, ng, 2, GV // rows, rows, 128), f32),
         pltpu.VMEM((groups, nta, 2, rows, 128), f32),
-        pltpu.VMEM((ng, 2, ng, 2, GV // rows, rows, 128), f32),
+        pltpu.VMEM((groups, nta, 2, rows, 128), f32),
+        pltpu.VMEM((ng, 2, nta, 2, rows, 128), f32),
         pltpu.VMEM((ng, nta, 2, rows, 128), f32),
         pltpu.VMEM((6, 8, nv), f32),
         dma((groups,)), dma((groups,)), dma((groups,)), dma((groups // 2,)),

time: 72.8 us -> 70.9 us (0.974)
  Pallas kernels: 69 us -> 66.8 us
    pallas_call x1, Pallas kernels: 69 us -> 66.8 us  [body(): pl.pallas_call(functools.partial(kernel, n, nta, 1.0 / math.sqrt(count),...]
where the time goes in v3:
time: 70.9 us; the launch traced here: 70.4 us
  Pallas kernels  66.8 us (94%)
  local copies, waits for them, and re-layouts  2.98 us (4%)
    pallas_call x1, Pallas kernels, body(): pl.pallas_call(functools.partial(kernel, n, nta, 1.0 / math.sqrt(count),...  66.8 us
    unnamed x7, local copies, waits for them, and re-layouts  2.98 us

profile of v3, /device:TPU:0, one launch (start us, length us, event | category | flops | bytes accessed | tf_op | source)
XLA Modules:
  0.0 70.4 jit_solution(8831362416363401622)
XLA Ops:
  0.6 0.0 copy-start
  0.6 0.0 copy-start.1
  0.6 1.4 %copy.5 = bf16[1,256,2,3,1,384]{5,1,3,2,4,0:T(8,128)(2,1)S(1)} copy(bf16[1,256,2,3,1,384]{5,2,4,3,1,0:T(2,128)(2,1)} %param.3) | data formatting | bytes 2359296 | tf_op args[0]
  2.1 0.0 copy-done
  2.1 0.0 copy-done.1
  2.1 66.8 %shard_map.50 = (f32[8,4,8,8,128]{4,3,2,1,0:T(8,128)S(1)}, f32[1,256]{1,0:T(1,128)S(1)}) custom-call(s32[4]{0:T(128)S(1)} %copy-done.1, s32[3,8]{1,0:T(4,128)S(1)} %bitcast.5, bf16[6,4,64,384]{3,2,1,0:T(8,128)(2,1)S(1)} %bitcast.4), custom_call_target="tpu_custom_call" | custom-call | tf_op jit(solution)/shard_map/pallas_call | solution.py:800
  68.9 1.0 %copy.8 = f32[8,4,8,8,128]{4,3,2,1,0:T(8,128)} copy(f32[8,4,8,8,128]{4,3,2,1,0:T(8,128)S(1)} %get-tuple-element.4) | data formatting | bytes 2097152
  69.9 0.6 copy.9
Async XLA Ops:
  0.6 1.5 %copy-start = (s32[8,3]{0,1:T(4,128)S(1)}, s32[8,3]{0,1:T(4,128)}, u32[]{:S(2)}) copy-start(s32[8,3]{0,1:T(4,128)} %param.4) | copy-start | bytes 292
  0.6 1.5 %copy-start.1 = (s32[4]{0:T(128)S(1)}, s32[4]{0:T(128)}, u32[]{:S(2)}) copy-start(s32[4]{0:T(128)} %order_ref.1) | copy-start | bytes 52

commit v4 on v3

--- a/solution.py
+++ b/solution.py
@@ -655,7 +655,21 @@
             send_b(s)
             return carry
 
-        lax.fori_loop(first_groups, groups - ng, second_step, 0)
+        def last_b(s, carry):
+            take_b(s)
+            return carry
+
+        def catch_up_all(later, odd_first, done):
+            def catch_up(q, carry):
+                odd = 2 * q + odd_first
+                slot = later * (first_groups + q) + (1 - later) * odd
+                before = later * second(first_groups + q, hi) + (1 - later) * first(odd, hi)
+                field[before, at(row1, wide, wide)] += times(lend[at(row1, wide, wide), :], rend[slot])
+                if done:
+                    finish(before, field[before, at(row1, wide, wide)])
+                return carry
+
+            lax.fori_loop(0, ng, catch_up, 0)
 
         def third_step(s, carry):
             step = s - (groups - ng)
@@ -672,9 +686,9 @@
             def _():
                 take_a(s - 2)
 
-            @pl.when(step >= 2)
-            def _():
-                take_b(s - 6)
+            @pl.when(step < 2)
+            def _():
+                lax.fori_loop(2 * s - 2 * first_groups, 2 * s - 2 * first_groups + 2, last_b, 0)
 
             group = far_rows(s, False)
             straight_a(s)
@@ -683,27 +697,14 @@
             near = lend[at(row1, wide, wide), :]
             finish(group, field[group, at(row1, wide, wide)] + times(near, rend[s]))
 
-            @pl.when(step < ng - 1)
-            def _():
-                later = (2 - step) // 2
-
-                def catch_up(q, carry):
-                    odd = 2 * q + 2 - step
-                    slot = later * (first_groups + q) + (1 - later) * odd
-                    before = later * second(first_groups + q, hi) + (1 - later) * first(odd, hi)
-                    field[before, at(row1, wide, wide)] += times(lend[at(row1, wide, wide), :], rend[slot])
-
-                    @pl.when(step != 1)
-                    def _():
-                        finish(before, field[before, at(row1, wide, wide)])
-                    return carry
-
-                lax.fori_loop(0, ng, catch_up, 0)
-            return carry
-
+            @pl.when(step < 2)
+            def _():
+                catch_up_all(1 - step, 1 - step, True)
+            return carry
+
+        lax.fori_loop(first_groups, groups - ng, second_step, 0)
+        catch_up_all(0, 1, False)
         lax.fori_loop(groups - ng, groups, third_step, 0)
-        take_b(groups - 6)
-        take_b(groups - 5)
 
         def put(m, carry):
             assemble(blk(m, hi), False)

time: 70.9 us -> 70.6 us (level)
  no operation moved by 1% of the time
where the time goes in v4:
time: 70.6 us; the launch traced here: 70.4 us
  Pallas kernels  66.8 us (95%)
  local copies, waits for them, and re-layouts  2.98 us (4%)
    pallas_call x1, Pallas kernels, body(): pl.pallas_call(functools.partial(kernel, n, nta, 1.0 / math.sqrt(count),...  66.8 us
    unnamed x7, local copies, waits for them, and re-layouts  2.98 us

profile of v4, /device:TPU:0, one launch (start us, length us, event | category | flops | bytes accessed | tf_op | source)
XLA Modules:
  0.0 70.4 jit_solution(2995514939328678790)
XLA Ops:
  0.6 0.0 copy-start
  0.6 0.0 copy-start.1
  0.6 1.4 %copy.5 = bf16[1,256,2,3,1,384]{5,1,3,2,4,0:T(8,128)(2,1)S(1)} copy(bf16[1,256,2,3,1,384]{5,2,4,3,1,0:T(2,128)(2,1)} %param.3) | data formatting | bytes 2359296 | tf_op args[0]
  2.1 0.0 copy-done
  2.1 0.0 copy-done.1
  2.1 66.8 %shard_map.50 = (f32[8,4,8,8,128]{4,3,2,1,0:T(8,128)S(1)}, f32[1,256]{1,0:T(1,128)S(1)}) custom-call(s32[4]{0:T(128)S(1)} %copy-done.1, s32[3,8]{1,0:T(4,128)S(1)} %bitcast.5, bf16[6,4,64,384]{3,2,1,0:T(8,128)(2,1)S(1)} %bitcast.4), custom_call_target="tpu_custom_call" | custom-call | tf_op jit(solution)/shard_map/pallas_call | solution.py:801
  68.9 1.0 %copy.8 = f32[8,4,8,8,128]{4,3,2,1,0:T(8,128)} copy(f32[8,4,8,8,128]{4,3,2,1,0:T(8,128)S(1)} %get-tuple-element.4) | data formatting | bytes 2097152
  69.9 0.6 copy.9
Async XLA Ops:
  0.6 1.5 %copy-start = (s32[8,3]{0,1:T(4,128)S(1)}, s32[8,3]{0,1:T(4,128)}, u32[]{:S(2)}) copy-start(s32[8,3]{0,1:T(4,128)} %param.4) | copy-start | bytes 292
  0.6 1.5 %copy-start.1 = (s32[4]{0:T(128)S(1)}, s32[4]{0:T(128)}, u32[]{:S(2)}) copy-start(s32[4]{0:T(128)} %order_ref.1) | copy-start | bytes 52

commit v5 on v4

--- a/solution.py
+++ b/solution.py
@@ -690,10 +690,11 @@
             def _():
                 lax.fori_loop(2 * s - 2 * first_groups, 2 * s - 2 * first_groups + 2, last_b, 0)
 
-            group = far_rows(s, False)
-            straight_a(s)
-
-            straight_b(s)
+            group = second(s, hi)
+            arrive(s, group, False)
+            for row, send in ((row3, straight_a), (row2, straight_b)):
+                field[group, at(row, wide, wide)] += times(lend[at(row, wide, wide), :], rend[s])
+                send(s)
             near = lend[at(row1, wide, wide), :]
             finish(group, field[group, at(row1, wide, wide)] + times(near, rend[s]))
 

time: 70.6 us -> 70.6 us (level)
  no operation moved by 1% of the time
where the time goes in v5:
time: 70.6 us; the launch traced here: 70.4 us
  Pallas kernels  66.8 us (95%)
  local copies, waits for them, and re-layouts  2.98 us (4%)
    pallas_call x1, Pallas kernels, body(): pl.pallas_call(functools.partial(kernel, n, nta, 1.0 / math.sqrt(count),...  66.8 us
    unnamed x7, local copies, waits for them, and re-layouts  2.98 us

profile of v5, /device:TPU:0, one launch (start us, length us, event | category | flops | bytes accessed | tf_op | source)
XLA Modules:
  0.0 70.4 jit_solution(10755181578924565467)
XLA Ops:
  0.6 0.0 copy-start
  0.6 0.0 copy-start.1
  0.6 1.4 %copy.5 = bf16[1,256,2,3,1,384]{5,1,3,2,4,0:T(8,128)(2,1)S(1)} copy(bf16[1,256,2,3,1,384]{5,2,4,3,1,0:T(2,128)(2,1)} %param.3) | data formatting | bytes 2359296 | tf_op args[0]
  2.1 0.0 copy-done
  2.1 0.0 copy-done.1
  2.1 66.8 %shard_map.50 = (f32[8,4,8,8,128]{4,3,2,1,0:T(8,128)S(1)}, f32[1,256]{1,0:T(1,128)S(1)}) custom-call(s32[4]{0:T(128)S(1)} %copy-done.1, s32[3,8]{1,0:T(4,128)S(1)} %bitcast.5, bf16[6,4,64,384]{3,2,1,0:T(8,128)(2,1)S(1)} %bitcast.4), custom_call_target="tpu_custom_call" | custom-call | tf_op jit(solution)/shard_map/pallas_call | solution.py:802
  68.9 1.0 %copy.8 = f32[8,4,8,8,128]{4,3,2,1,0:T(8,128)} copy(f32[8,4,8,8,128]{4,3,2,1,0:T(8,128)S(1)} %get-tuple-element.4) | data formatting | bytes 2097152
  69.9 0.6 copy.9
Async XLA Ops:
  0.6 1.5 %copy-start = (s32[8,3]{0,1:T(4,128)S(1)}, s32[8,3]{0,1:T(4,128)}, u32[]{:S(2)}) copy-start(s32[8,3]{0,1:T(4,128)} %param.4) | copy-start | bytes 292
  0.6 1.5 %copy-start.1 = (s32[4]{0:T(128)S(1)}, s32[4]{0:T(128)}, u32[]{:S(2)}) copy-start(s32[4]{0:T(128)} %order_ref.1) | copy-start | bytes 52
